TPU v7x, 128 devices: a whole 4x4x4 slice. The times are simulated.
128 devices in a mesh: aa: 16 (over x, z_hi, core), ba: 8 (over y, z_lo).
Axes of the slice: x: 4, y: 4, z: 4 (z_hi: 2, z_lo: 2; z = z_hi * 2 + z_lo), core: 2. Of those that a mesh axis runs over, the one named last changes fastest.
Arguments:
- amplitudes: bfloat16 [2048, 2048], P('aa', 'ba'), may hold values from -6 to 6
- code: int32 [32, 2048], replicated, may hold values from -2048 to 2048, as said below
- counts: int32 [128], replicated, may hold values from 1 to 16, as said below
- pair_irrep: int32 [32], replicated, may hold values from 0 to 7
- integrals: bfloat16 [32, 32], replicated, may hold values from -3 to 3
- one_body: bfloat16 [32], replicated, may hold values from -1.5 to 1.5
Outputs:
- sigma: bfloat16 [2048, 2048], P('aa', 'ba')
Inputs may be any that keep to these rules, and one draw needn't show every extreme that they name: |code| - 1 names the target string of a replacement and the sign of code its sign; some entries reach both ends. `counts`: the live strings of fine block j fill its first slots, from slot j * 16 on; in every draw some block is full and some holds one string.
All inputs are finite; a program needn't handle non-finite values.
Results may differ from a plain program's by a relative error of at most 0.0045.
Values may be sent and summed in bfloat16 or wider, within the bound.
A program may use at most 128 MiB of HBM per device.

v0:
```python
import jax
import jax.numpy as jnp
from jax import lax
from jax.sharding import PartitionSpec as P


def one_hot(tables, signs, first, width):
    ids = first + jnp.arange(width, dtype=jnp.int32)
    return jnp.where(
        tables[:, :, None] == ids[None, None, :], signs[:, :, None], jnp.zeros((), jnp.bfloat16)
    )


def alpha_term(tables, signs, values, start_a, rows_a, rows_b, count):
    groups = tables.shape[0] // 8
    rows_t = tables.reshape(groups, 8, count)
    rows_s = signs.reshape(groups, 8, count)

    def one_group(carry, items):
        tab, sgn, val = items
        hot = one_hot(tab, sgn, start_a, rows_a)
        return (
            carry + jnp.einsum("prk,pkb->rb", hot, val, preferred_element_type=jnp.float32),
            None,
        )

    total, _ = lax.scan(
        one_group,
        jnp.zeros((count, rows_b), jnp.float32),
        (rows_t, rows_s, values.reshape(groups, 8, rows_a, rows_b)),
    )
    return total


def per_device(amplitudes, code, counts, pair_irrep, integrals, one_body):
    rows_a, rows_b = amplitudes.shape
    pairs, strings = code.shape
    groups = pairs // 8
    capacity = strings // counts.shape[0]
    slots = jnp.arange(strings, dtype=jnp.int32)
    live_all = (slots % capacity < jnp.repeat(counts, capacity)).astype(jnp.bfloat16)
    start_a = lax.axis_index("aa") * rows_a
    start_b = lax.axis_index("ba") * rows_b
    live_a = lax.dynamic_slice_in_dim(live_all, start_a, rows_a)
    live_b = lax.dynamic_slice_in_dim(live_all, start_b, rows_b)
    masked = amplitudes * (live_a[:, None] * live_b[None, :])
    target = jnp.abs(code) - 1
    signs = jnp.sign(code).astype(jnp.bfloat16)
    target_a = lax.dynamic_slice_in_dim(target, start_a, rows_a, 1).reshape(groups, 8, rows_a)
    signs_a = lax.dynamic_slice_in_dim(signs, start_a, rows_a, 1).reshape(groups, 8, rows_a)
    target_b = lax.dynamic_slice_in_dim(target, start_b, rows_b, 1).reshape(groups, 8, rows_b)
    signs_b = lax.dynamic_slice_in_dim(signs, start_b, rows_b, 1).reshape(groups, 8, rows_b)
    piece = lax.all_gather(masked, "ba", axis=1, tiled=True)
    start = jnp.int32(0)

    def one_group(items):
        tab, sgn = items
        hot = one_hot(tab, sgn, start, piece.shape[1])
        return jnp.einsum("pkc,ic->pik", hot, piece, preferred_element_type=jnp.float32)

    beta_sum = lax.map(one_group, (target_b, signs_b)).reshape(pairs, rows_a, rows_b)
    dbeta = (beta_sum * live_b[None, None, :]).astype(jnp.bfloat16)
    alpha_piece = lax.all_gather(masked, "aa", axis=0, tiled=True)
    alpha_start = jnp.int32(0)

    def one_group(items):
        tab, sgn = items
        hot = one_hot(tab, sgn, alpha_start, alpha_piece.shape[0])
        return jnp.einsum("pkj,jb->pkb", hot, alpha_piece, preferred_element_type=jnp.float32)

    alpha_sum = lax.map(one_group, (target_a, signs_a)).reshape(pairs, rows_a, rows_b)
    dalpha = (alpha_sum * live_a[None, :, None]).astype(jnp.bfloat16)
    weights = jnp.where(
        pair_irrep[:, None] == pair_irrep[None, :], integrals, jnp.zeros((), jnp.bfloat16)
    )
    gbeta_full = jnp.einsum("pq,qik->pik", weights, dbeta, preferred_element_type=jnp.float32)
    galpha_full = jnp.einsum("pq,qik->pik", weights, dalpha, preferred_element_type=jnp.float32)
    gbeta = gbeta_full.astype(jnp.bfloat16)
    combined = (gbeta_full + 0.5 * galpha_full).astype(jnp.bfloat16)
    local = jnp.einsum("p,pik->ik", one_body, dbeta, preferred_element_type=jnp.float32)
    local = local + jnp.einsum("p,pik->ik", one_body, dalpha, preferred_element_type=jnp.float32)
    half_beta = gbeta * 0.5
    gathered_piece = lax.all_gather(half_beta, "ba", axis=2, tiled=True)
    gathered_start = jnp.int32(0)
    width = gathered_piece.shape[2]

    def one_group(acc, items):
        tab, sgn, val = items
        hot = one_hot(tab, sgn, gathered_start, width)
        return (acc + jnp.einsum("pbk,pak->ab", hot, val, preferred_element_type=jnp.float32), None)

    total, _ = lax.scan(
        one_group,
        jnp.zeros((rows_a, rows_b), jnp.float32),
        (target_b, signs_b, gathered_piece.reshape(groups, 8, rows_a, width)),
    )
    beta_part = total
    alpha_rows = lax.psum_scatter(
        alpha_term(target, signs, combined, start_a, rows_a, rows_b, lax.axis_size("aa") * rows_a),
        "aa",
        scatter_dimension=0,
        tiled=True,
    )
    total = local + beta_part + alpha_rows
    return (total * (live_a[:, None] * live_b[None, :])).astype(jnp.bfloat16)


def solution(mesh):
    placed = (P("aa", "ba"), P(), P(), P(), P(), P())
    return jax.shard_map(
        per_device, mesh=mesh, in_specs=placed, out_specs=P("aa", "ba"), check_vma=False
    )
```

profile of v0, /device:TPU:0, one launch (start us, length us, event | category | flops | bytes accessed | tf_op | source)
XLA Modules:
  0.0 478.1 jit_solution(13989300065784865499)
XLA Ops:
  6.5 0.7 broadcast_in_dim.92
  7.3 0.1 reshape.63
  7.4 0.1 fusion.73
  7.5 0.1 fusion.74
  7.5 1.6 multiply_multiply_fusion
  9.2 29.7 %all_gather.9 = bf16[128,2048]{1,0:T(8,128)(2,1)S(1)} all-gather(bf16[128,256]{1,0:T(8,128)(2,1)} %multiply_multiply_fusion), channel_id=1, replica_groups=mesh['aa'=16,'ba'=8] {'ba'}, dimensions={1}, use_global_device_ids=true | all-gather | bytes 589824 | tf_op jit(solution)/shard_map/all_gather | solution.py:53
  38.9 1.0 abs_add_fusion
  40.0 13.7 %while.42 = (s32[]{:T(128)}, f32[4,8,128,256]{2,3,1,0:T(8,128)}, s32[4,8,256]{2,1,0:T(8,128)S(1)}, bf16[4,8,256]{2,1,0:T(8,128)(2,1)S(1)}, bf16[128,2048]{1,0:T(8,128)(2,1)S(1)}, /*index=5*/s32[]{:T(128)}) while((s32[]{:T(128)}, f32[4,8,128,256]{2,3,1,0:T(8,128)}, s32[4,8,256]{2,1,0:T(8,128)S(1)}, bf16[4,8,256]{2,1,0:T(8,128)(2,1)S(1)}, ...), condition=%wide.region_1.2_spmd, body=%wide.region_0.1_spmd.sunk | while | flops 1082130432 | bytes 1609817 | solution.py:61
  40.0 3.4 fusion.91
  43.4 3.4 fusion.91
  46.9 3.4 fusion.91
  50.3 3.4 fusion.91
  53.7 5.5 %copy.13 = f32[32,128,256]{2,0,1:T(8,128)} copy(f32[32,128,256]{1,2,0:T(8,128)} %bitcast.130) | data formatting | bytes 8388608 | tf_op jit(solution)/shard_map/reshape | solution.py:61
  59.2 5.5 %convert_multiply_fusion = (bf16[32,128,256]{2,0,1:T(8,128)(2,1)}, f32[32,128,256]{2,0,1:T(8,128)}) fusion(f32[32,128,256]{2,0,1:T(8,128)} %copy.13, f32[256]{0:T(256)S(1)} %get-tuple-element.237, bf16[32,32]{1,0:T(8,128)(2,1)S(1)} %copy-done.2, s32[32]{0:T(128)S(1)} %copy-done.3), kind=kOutput, calls=%fused_computation.55 | convolution fusion | flops 71305216 | bytes 10488960 | tf_op jit(solution)/shard_map/pq,qik->pik/dot_general | solution.py:76
  64.8 0.0 reduce-scatter.2.cloned.1.call-start
  64.9 2.6 fusion.52
  67.5 14.2 %while.43 = (s32[]{:T(128)}, f32[4,8,128,256]{3,2,1,0:T(8,128)}, s32[4,8,128]{2,1,0:T(8,128)S(1)}, bf16[4,8,128]{2,1,0:T(8,128)(2,1)S(1)}, bf16[2048,256]{1,0:T(8,128)(2,1)}, /*index=5*/s32[]{:T(128)}) while((s32[]{:T(128)}, f32[4,8,128,256]{3,2,1,0:T(8,128)}, s32[4,8,128]{2,1,0:T(8,128)S(1)}, bf16[4,8,128]{2,1,0:T(8,128)(2,1)S(1)}, ...), condition=%wide.region_3.4_spmd, body=%wide.region_2.3_spmd.sunk | while | flops 1077936128 | bytes 2115673 | solution.py:71
  67.6 3.6 fusion.94
  71.2 3.5 fusion.94
  74.7 3.5 fusion.94
  78.2 3.5 fusion.94
  81.7 4.8 %fusion.65 = f32[1,128,256]{2,0,1:T(1,128)S(1)} fusion(bf16[32]{0:T(256)(128)(2,1)S(1)} %copy-done, f32[32,128,256]{2,1,0:T(8,128)} %bitcast.128, f32[128]{0:T(128)S(1)} %get-tuple-element.235), kind=kOutput, calls=%fused_computation.80 | convolution fusion | flops 4194304 | bytes 4325952 | tf_op jit(solution)/shard_map/p,pik->ik/dot_general | solution.py:81
  86.5 4.9 %fusion.50 = bf16[4,8,128,256]{3,1,0,2:T(8,128)(2,1)S(1)} fusion(f32[32,128,256]{2,0,1:T(8,128)S(1)} %copy-done.1, bf16[32,32]{1,0:T(8,128)(2,1)S(1)} %copy-done.2, s32[32]{0:T(128)S(1)} %copy-done.3, f32[32,128,256]{2,1,0:T(8,128)} %bitcast.129, f32[128]{0:T(128)S(1)} %get-tuple-element.235), kind=kOutput, calls=%fused_computation.56 | convolution fusion | flops 72353792 | bytes 10488448 | tf_op jit(solution)/shard_map/pq,qik->pik/dot_general | solution.py:77
  91.4 27.8 %while.45 = (s32[]{:T(128)}, f32[2048,256]{1,0:T(8,128)}, s32[4,8,2048]{2,1,0:T(8,128)S(1)}, s32[]{:T(128)}, bf16[4,8,2048]{2,1,0:T(8,128)(2,1)S(1)}, /*index=5*...) while((s32[]{:T(128)}, f32[2048,256]{1,0:T(8,128)}, s32[4,8,2048]{2,1,0:T(8,128)S(1)}, ...), condition=%wide.region_7.8_spmd.clone, body=%wide.region_6.7_spmd.clone.sunk | while | flops 1078984832 | bytes 6063223 | solution.py:27
  91.5 0.1 constant_dynamic-slice_fusion.5
  91.6 6.1 %fusion.98 = f32[2048,256]{1,0:T(8,128)} fusion(s32[128]{0:T(128)S(1)} %iota_add_fusion.2, s32[8,2048]{1,0:T(8,128)S(1)} %dynamic-slice_bitcast_fusion.26, f32[2048,256]{1,0:T(8,128)} %get-tuple-element.419, bf16[8,2048]{1,0:T(8,128)(2,1)S(1)} %dynamic-slice_bitcast_fusion.27, pred[]{:T(512)S(6)} %compare.8, ...), kind=kOutput, calls=%fused_computation.42.clone.1 | convolution fusion | flops 1078984704 | bytes 4817409 | tf_op jit(solution)/shard_map/while/body/eval_jaxpr/prk,pkb->rb/dot_general | solution.py:23
  97.7 0.1 constant_dynamic-slice_fusion.5
  97.8 7.1 %fusion.98 = f32[2048,256]{1,0:T(8,128)} fusion(s32[128]{0:T(128)S(1)} %iota_add_fusion.2, s32[8,2048]{1,0:T(8,128)S(1)} %dynamic-slice_bitcast_fusion.26, f32[2048,256]{1,0:T(8,128)} %get-tuple-element.419, bf16[8,2048]{1,0:T(8,128)(2,1)S(1)} %dynamic-slice_bitcast_fusion.27, pred[]{:T(512)S(6)} %compare.8, ...), kind=kOutput, calls=%fused_computation.42.clone.1 | convolution fusion | flops 1078984704 | bytes 4817409 | tf_op jit(solution)/shard_map/while/body/eval_jaxpr/prk,pkb->rb/dot_general | solution.py:23
  104.8 0.1 constant_dynamic-slice_fusion.5
  104.9 7.1 %fusion.98 = f32[2048,256]{1,0:T(8,128)} fusion(s32[128]{0:T(128)S(1)} %iota_add_fusion.2, s32[8,2048]{1,0:T(8,128)S(1)} %dynamic-slice_bitcast_fusion.26, f32[2048,256]{1,0:T(8,128)} %get-tuple-element.419, bf16[8,2048]{1,0:T(8,128)(2,1)S(1)} %dynamic-slice_bitcast_fusion.27, pred[]{:T(512)S(6)} %compare.8, ...), kind=kOutput, calls=%fused_computation.42.clone.1 | convolution fusion | flops 1078984704 | bytes 4817409 | tf_op jit(solution)/shard_map/while/body/eval_jaxpr/prk,pkb->rb/dot_general | solution.py:23
  112.0 0.1 constant_dynamic-slice_fusion.5
  112.1 7.1 %fusion.98 = f32[2048,256]{1,0:T(8,128)} fusion(s32[128]{0:T(128)S(1)} %iota_add_fusion.2, s32[8,2048]{1,0:T(8,128)S(1)} %dynamic-slice_bitcast_fusion.26, f32[2048,256]{1,0:T(8,128)} %get-tuple-element.419, bf16[8,2048]{1,0:T(8,128)(2,1)S(1)} %dynamic-slice_bitcast_fusion.27, pred[]{:T(512)S(6)} %compare.8, ...), kind=kOutput, calls=%fused_computation.42.clone.1 | convolution fusion | flops 1078984704 | bytes 4817409 | tf_op jit(solution)/shard_map/while/body/eval_jaxpr/prk,pkb->rb/dot_general | solution.py:23
  119.2 274.2 %all-gather.5.cloned.1.call-done = bf16[32,128,2048]{2,0,1:T(8,128)(2,1)} async-done(((bf16[32,128,256]{2,0,1:T(8,128)(2,1)}), bf16[32,128,2048]{2,0,1:T(8,128)(2,1)}) %all-gather.5.cloned.1.call-update) | async-done | bytes 16777232 | tf_op jit(solution)/shard_map/all_gather | solution.py:83
  393.4 40.3 %while.44 = (s32[]{:T(128)}, f32[128,256]{1,0:T(8,128)S(1)}, bf16[4,8,128,2048]{3,1,0,2:T(8,128)(2,1)}, s32[4,8,256]{2,1,0:T(8,128)S(1)}, bf16[4,8,256]{2,1,0:T(8,128)(2,1)S(1)}, /*index=5*/s32[]{:T(128)}, s32[]{:T(128)}) while((s32[]{:T(128)}, f32[128,256]{1,0:T(8,128)S(1)}, bf16[4,8,128,2048]{3,1,0,2:T(8,128)(2,1)}, ...), condition=%wide.region_5.6_spmd.clone, body=%wide.region_4.5_spmd.clone.sunk | while | flops 1082195968 | bytes 29659240 | solution.py:92
  393.4 2.5 constant_dynamic-slice_fusion.4
  395.9 2.0 fusion.96
  397.9 5.5 %fusion.97 = f32[128,256]{1,0:T(8,128)S(1)} fusion(bf16[1,8,128,2048]{3,1,0,2:T(8,128)(2,1)S(1)} %constant_dynamic-slice_fusion.4, f32[128,256]{1,0:T(8,128)S(1)} %get-tuple-element.442, pred[]{:T(512)S(6)} %compare.7, bf16[8,256,2048]{2,1,0:T(8,128)(2,1)S(1)} %fusion.96), kind=kOutput, calls=%fused_computation.32.clone.2 | convolution fusion | flops 1073807360 | bytes 12845057 | tf_op jit(solution)/shard_map/while/body/eval_jaxpr/pbk,pak->ab/dot_general | solution.py:90
  403.5 2.5 constant_dynamic-slice_fusion.4
  406.0 2.0 fusion.96
  408.0 5.5 %fusion.97 = f32[128,256]{1,0:T(8,128)S(1)} fusion(bf16[1,8,128,2048]{3,1,0,2:T(8,128)(2,1)S(1)} %constant_dynamic-slice_fusion.4, f32[128,256]{1,0:T(8,128)S(1)} %get-tuple-element.442, pred[]{:T(512)S(6)} %compare.7, bf16[8,256,2048]{2,1,0:T(8,128)(2,1)S(1)} %fusion.96), kind=kOutput, calls=%fused_computation.32.clone.2 | convolution fusion | flops 1073807360 | bytes 12845057 | tf_op jit(solution)/shard_map/while/body/eval_jaxpr/pbk,pak->ab/dot_general | solution.py:90
  413.6 2.6 constant_dynamic-slice_fusion.4
  416.2 2.0 fusion.96
  418.2 5.5 %fusion.97 = f32[128,256]{1,0:T(8,128)S(1)} fusion(bf16[1,8,128,2048]{3,1,0,2:T(8,128)(2,1)S(1)} %constant_dynamic-slice_fusion.4, f32[128,256]{1,0:T(8,128)S(1)} %get-tuple-element.442, pred[]{:T(512)S(6)} %compare.7, bf16[8,256,2048]{2,1,0:T(8,128)(2,1)S(1)} %fusion.96), kind=kOutput, calls=%fused_computation.32.clone.2 | convolution fusion | flops 1073807360 | bytes 12845057 | tf_op jit(solution)/shard_map/while/body/eval_jaxpr/pbk,pak->ab/dot_general | solution.py:90
  423.7 2.5 constant_dynamic-slice_fusion.4
  426.2 2.0 fusion.96
  428.2 5.5 %fusion.97 = f32[128,256]{1,0:T(8,128)S(1)} fusion(bf16[1,8,128,2048]{3,1,0,2:T(8,128)(2,1)S(1)} %constant_dynamic-slice_fusion.4, f32[128,256]{1,0:T(8,128)S(1)} %get-tuple-element.442, pred[]{:T(512)S(6)} %compare.7, bf16[8,256,2048]{2,1,0:T(8,128)(2,1)S(1)} %fusion.96), kind=kOutput, calls=%fused_computation.32.clone.2 | convolution fusion | flops 1073807360 | bytes 12845057 | tf_op jit(solution)/shard_map/while/body/eval_jaxpr/pbk,pak->ab/dot_general | solution.py:90
  433.8 36.2 %reduce-scatter.2.cloned.1.call-done = f32[128,256]{1,0:T(8,128)} async-done(((f32[2048,256]{1,0:T(8,128)}), f32[128,256]{1,0:T(8,128)}) %reduce-scatter.2.cloned.1.call-update) | async-done | bytes 131088 | tf_op jit(solution)/shard_map/reduce_scatter | solution.py:98
  470.0 1.6 fusion.56
  (59 shorter events, 0.4 us)
Async XLA Ops:
  6.5 58.4 %copy-start = (bf16[32]{0:T(256)(128)(2,1)S(1)}, bf16[32]{0:T(256)(128)(2,1)}, u32[]{:S(2)}) copy-start(bf16[32]{0:T(256)(128)(2,1)} %param.19) | copy-start | bytes 196
  6.5 61.0 %all-gather.3.cloned.1.call-start = ((), (), s32[]{:S(2)}) async-start(), calls=%async_computation.1 | async-start | bytes 1114112 | tf_op jit(solution)/shard_map/all_gather | solution.py:63
  9.1 384.3 %all-gather.5.cloned.1.call-start = ((), (), s32[]{:S(2)}) async-start(), calls=%async_computation.2 | async-start | bytes 18874368 | tf_op jit(solution)/shard_map/all_gather | solution.py:83
  53.7 5.5 %copy-start.2 = (bf16[32,32]{1,0:T(8,128)(2,1)S(1)}, bf16[32,32]{1,0:T(8,128)(2,1)}, u32[]{:S(2)}) copy-start(bf16[32,32]{1,0:T(8,128)(2,1)} %param.18) | copy-start | bytes 6148
  53.7 5.5 %copy-start.3 = (s32[32]{0:T(128)S(1)}, s32[32]{0:T(128)}, u32[]{:S(2)}) copy-start(s32[32]{0:T(128)} %param.17) | copy-start | bytes 388
  64.8 405.2 %reduce-scatter.2.cloned.1.call-start = ((), (), s32[]{:S(2)}) async-start(), calls=%async_computation.3 | async-start | bytes 2228224 | tf_op jit(solution)/shard_map/reduce_scatter | solution.py:98
  81.7 4.8 %copy-start.1 = (f32[32,128,256]{2,0,1:T(8,128)S(1)}, f32[32,128,256]{2,0,1:T(8,128)}, u32[]{:S(2)}) copy-start(f32[32,128,256]{2,0,1:T(8,128)} %get-tuple-element.243) | copy-start | bytes 12582916
Sparse Core Ops, SparseCore 0:
  9.7 47.5 all-gather.2
  64.9 328.4 all-gather.4
  397.4 72.5 reduce-scatter.1
where the time goes:
time: 479 us; the launch traced here: 478 us
  waiting for transfers between devices  310 us (65%)
  matrix products  94.9 us (20%)
  blocking collectives  29.7 us (6%)
  local copies, waits for them, and re-layouts  17 us (4%)
  between operations  13.2 us (3%)
  other arithmetic  12.3 us (3%)
    all_gather x1, waiting for transfers between devices, per_device(): gathered_piece = lax.all_gather(half_beta, 'ba', axis=2, tiled=True)  274 us
    reduce_scatter x1, waiting for transfers between devices, per_device(): lax.psum_scatter(alpha_term(target, signs, combined, start_a, rows_a, row...  36.2 us
    all_gather x1, blocking collectives, per_device(): piece = lax.all_gather(masked, 'ba', axis=1, tiled=True)  29.7 us
    dot_general x4, matrix products, one_group(): jnp.einsum('prk,pkb->rb', hot, val, preferred_element_type=jnp.float32)  27.3 us
    dot_general x4, matrix products, one_group(): jnp.einsum('pbk,pak->ab', hot, val, preferred_element_type=jnp.float32)  22 us
    dot_general x4, matrix products, one_group(): jnp.einsum('pkj,jb->pkb', hot, alpha_piece, preferred_element_type=jnp.fl...  14.1 us
    dot_general x4, matrix products, one_group(): jnp.einsum('pkc,ic->pik', hot, piece, preferred_element_type=jnp.float32)  13.7 us
    dynamic_slice x4, local copies, waits for them, and re-layouts, per_device(): lax.scan(one_group, jnp.zeros((rows_a, rows_b), jnp.float32), (target_b,...  10.1 us
  transfers between devices with their start and end apart: 3, of which 2 were waited for; matrix products, arithmetic and copies ran while one was open for 25% of the time, Pallas kernels for 0%

commit v1 on v0

--- a/solution.py
+++ b/solution.py
@@ -80,7 +80,10 @@
     local = jnp.einsum("p,pik->ik", one_body, dbeta, preferred_element_type=jnp.float32)
     local = local + jnp.einsum("p,pik->ik", one_body, dalpha, preferred_element_type=jnp.float32)
     half_beta = gbeta * 0.5
-    gathered_piece = lax.all_gather(half_beta, "ba", axis=2, tiled=True)
+    n_dev = lax.axis_size("ba")
+    tiles = jnp.stack([half_beta for _ in range(n_dev)])
+    tiles = lax.all_to_all(tiles, "ba", split_axis=0, concat_axis=0)
+    gathered_piece = jnp.concatenate(tiles, axis=2)
     gathered_start = jnp.int32(0)
     width = gathered_piece.shape[2]
 

time: 479 us -> 392 us (0.82)
  waiting for transfers between devices: 310 us -> 205 us
  local copies, waits for them, and re-layouts: 17 us -> 46.8 us
  matrix products: 94.9 us -> 85.5 us
  other arithmetic: 12.3 us -> 3.76 us
  starting transfers between devices: 0.09 us -> 6.01 us
    all_gather x1 -> x0, waiting for transfers between devices: 274 us -> none  [per_device(): gathered_piece = lax.all_gather(half_beta, 'ba', axis=2, tiled=True)]
    all_gather x1, waiting for transfers between devices: 0.02 us -> 119 us  [per_device(): alpha_piece = lax.all_gather(masked, 'aa', axis=0, tiled=True)]
    all_to_all x0 -> x1, waiting for transfers between devices: none -> 48 us  [per_device(): tiles = lax.all_to_all(tiles, 'ba', split_axis=0, concat_axis=0)]
    all_to_all x0 -> x1, local copies, waits for them, and re-layouts: none -> 22.6 us  [per_device(): tiles = lax.all_to_all(tiles, 'ba', split_axis=0, concat_axis=0)]
    dot_general x0 -> x4, local copies, waits for them, and re-layouts: none -> 10.2 us  [one_group(): jnp.einsum('pbk,pak->ab', hot, val, preferred_element_type=jnp.float32)]
    dynamic_slice x4 -> x0, local copies, waits for them, and re-layouts: 10.1 us -> none  [per_device(): lax.scan(one_group, jnp.zeros((rows_a, rows_b), jnp.float32), (target_b,...]
    dot_general x4, matrix products: 22 us -> 12.6 us  [one_group(): jnp.einsum('pbk,pak->ab', hot, val, preferred_element_type=jnp.float32)]
    dot_general x4 -> x0, other arithmetic: 7.93 us -> none  [one_group(): jnp.einsum('pbk,pak->ab', hot, val, preferred_element_type=jnp.float32)]
  transfers between devices with their start and end apart: 3 -> 3, of which waited for: 2 -> 3; matrix products, arithmetic and copies ran while one was open for 25% -> 26% of each run, Pallas kernels for 0% -> 0%
where the time goes in v1:
time: 392 us; the launch traced here: 390 us
  waiting for transfers between devices  205 us (52%)
  matrix products  85.5 us (22%)
  local copies, waits for them, and re-layouts  46.8 us (12%)
  blocking collectives  29.6 us (8%)
  between operations  13.5 us (3%)
  starting transfers between devices  6.01 us (2%)
    all_gather x1, waiting for transfers between devices, per_device(): alpha_piece = lax.all_gather(masked, 'aa', axis=0, tiled=True)  119 us
    all_to_all x1, waiting for transfers between devices, per_device(): tiles = lax.all_to_all(tiles, 'ba', split_axis=0, concat_axis=0)  48 us
    reduce_scatter x1, waiting for transfers between devices, per_device(): lax.psum_scatter(alpha_term(target, signs, combined, start_a, rows_a, row...  37.4 us
    all_gather x1, blocking collectives, per_device(): piece = lax.all_gather(masked, 'ba', axis=1, tiled=True)  29.6 us
    dot_general x4, matrix products, one_group(): jnp.einsum('prk,pkb->rb', hot, val, preferred_element_type=jnp.float32)  27.1 us
    all_to_all x1, local copies, waits for them, and re-layouts, per_device(): tiles = lax.all_to_all(tiles, 'ba', split_axis=0, concat_axis=0)  22.6 us
    dot_general x4, matrix products, one_group(): jnp.einsum('pkj,jb->pkb', hot, alpha_piece, preferred_element_type=jnp.fl...  14 us
    dot_general x4, matrix products, one_group(): jnp.einsum('pkc,ic->pik', hot, piece, preferred_element_type=jnp.float32)  13.6 us
  transfers between devices with their start and end apart: 3, of which 3 were waited for; matrix products, arithmetic and copies ran while one was open for 26% of the time, Pallas kernels for 0%

profile of v1, /device:TPU:0, one launch (start us, length us, event | category | flops | bytes accessed | tf_op | source)
XLA Modules:
  0.0 390.3 jit_solution(12162741424288155000)
XLA Ops:
  6.5 0.7 broadcast_in_dim.92
  7.3 0.1 reshape.65
  7.4 0.1 fusion.80
  7.5 0.9 multiply_multiply_fusion
  8.5 29.6 %all_gather.6 = bf16[128,2048]{1,0:T(8,128)(2,1)S(1)} all-gather(bf16[128,256]{1,0:T(8,128)(2,1)S(1)} %multiply_multiply_fusion), channel_id=1, replica_groups=mesh['aa'=16,'ba'=8] {'ba'}, dimensions={1}, use_global_device_ids=true | all-gather | bytes 589824 | tf_op jit(solution)/shard_map/all_gather | solution.py:53
  38.1 1.0 abs_add_fusion
  39.2 13.7 %while.42 = (s32[]{:T(128)}, f32[4,8,128,256]{2,3,1,0:T(8,128)}, s32[4,8,256]{2,1,0:T(8,128)S(1)}, bf16[4,8,256]{2,1,0:T(8,128)(2,1)S(1)}, bf16[128,2048]{1,0:T(8,128)(2,1)S(1)}, /*index=5*/s32[]{:T(128)}) while((s32[]{:T(128)}, f32[4,8,128,256]{2,3,1,0:T(8,128)}, s32[4,8,256]{2,1,0:T(8,128)S(1)}, bf16[4,8,256]{2,1,0:T(8,128)(2,1)S(1)}, ...), condition=%wide.region_1.2_spmd, body=%wide.region_0.1_spmd.sunk | while | flops 1082130432 | bytes 1609817 | solution.py:61
  39.3 3.4 fusion.103
  42.7 3.4 fusion.103
  46.1 3.4 fusion.103
  49.5 3.4 fusion.103
  52.9 5.5 %copy.23 = f32[32,128,256]{2,0,1:T(8,128)} copy(f32[32,128,256]{1,2,0:T(8,128)} %bitcast.137) | data formatting | bytes 8388608 | tf_op jit(solution)/shard_map/reshape | solution.py:61
  58.4 5.0 %convert_multiply_fusion = (bf16[32,128,256]{2,0,1:T(8,128)(2,1)S(1)}, f32[32,128,256]{2,0,1:T(8,128)}) fusion(f32[32,128,256]{2,0,1:T(8,128)} %copy.23, f32[256]{0:T(256)S(1)} %get-tuple-element.254, bf16[32,32]{1,0:T(8,128)(2,1)S(1)} %copy-done.2, s32[32]{0:T(128)S(1)} %copy-done.3), kind=kOutput, calls=%fused_computation.56 | convolution fusion | flops 71305216 | bytes 10488960 | tf_op jit(solution)/shard_map/pq,qik->pik/dot_general | solution.py:76
  63.4 1.2 copy.25
  64.6 6.0 %stack.2 = bf16[8,32,128,256]{3,2,1,0:T(8,128)(2,1)} broadcast(bf16[32,128,256]{2,1,0:T(8,128)(2,1)S(1)} %copy.25), dimensions={1,2,3} | broadcast | bytes 18874368 | tf_op jit(solution)/shard_map/stack | solution.py:84
  70.6 5.7 %all-to-all-start = ((bf16[8,32,128,256]{3,2,1,0:T(8,128)(2,1)}), bf16[8,32,128,256]{3,2,1,0:T(8,128)(2,1)}, u32[]{:S(2)}, u32[]{:S(2)}) async-start(bf16[8,32,128,256]{3,2,1,0:T(8,128)(2,1)} %stack.2), calls=%async_computation | async-start | bytes 33554432 | tf_op jit(solution)/shard_map/all_to_all | solution.py:85
  76.4 0.7 all-gather.2.cloned.1.call-update
  77.1 0.2 reduce-scatter.2.cloned.1.call-start
  77.4 2.6 fusion.59
  80.0 118.6 %all-gather.2.cloned.1.call-done = bf16[2048,256]{1,0:T(8,128)(2,1)} async-done(((bf16[128,256]{1,0:T(8,128)(2,1)}), bf16[2048,256]{1,0:T(8,128)(2,1)}) %all-gather.2.cloned.1.call-update) | async-done | bytes 1048592 | tf_op jit(solution)/shard_map/all_gather | solution.py:63
  198.6 14.0 %while.43 = (s32[]{:T(128)}, f32[4,8,128,256]{3,2,1,0:T(8,128)}, s32[4,8,128]{2,1,0:T(8,128)S(1)}, bf16[4,8,128]{2,1,0:T(8,128)(2,1)S(1)}, bf16[2048,256]{1,0:T(8,128)(2,1)}, /*index=5*/s32[]{:T(128)}) while((s32[]{:T(128)}, f32[4,8,128,256]{3,2,1,0:T(8,128)}, s32[4,8,128]{2,1,0:T(8,128)S(1)}, bf16[4,8,128]{2,1,0:T(8,128)(2,1)S(1)}, ...), condition=%wide.region_3.4_spmd, body=%wide.region_2.3_spmd.sunk | while | flops 1077936128 | bytes 2115673 | solution.py:71
  198.6 3.5 fusion.106
  202.1 3.6 fusion.106
  205.7 3.5 fusion.106
  209.1 3.5 fusion.106
  212.6 6.0 %fusion.57 = bf16[4,8,128,256]{3,1,0,2:T(8,128)(2,1)S(1)} fusion(f32[32,128,256]{2,0,1:T(8,128)} %get-tuple-element.260, bf16[32,32]{1,0:T(8,128)(2,1)S(1)} %copy-done.2, s32[32]{0:T(128)S(1)} %copy-done.3, f32[32,128,256]{2,1,0:T(8,128)} %bitcast.135, f32[128]{0:T(128)S(1)} %get-tuple-element.252), kind=kOutput, calls=%fused_computation.57 | convolution fusion | flops 72353792 | bytes 10488448 | tf_op jit(solution)/shard_map/pq,qik->pik/dot_general | solution.py:77
  218.6 27.6 %while.45 = (s32[]{:T(128)}, f32[2048,256]{1,0:T(8,128)}, s32[4,8,2048]{2,1,0:T(8,128)S(1)}, s32[]{:T(128)}, bf16[4,8,2048]{2,1,0:T(8,128)(2,1)S(1)}, /*index=5*...) while((s32[]{:T(128)}, f32[2048,256]{1,0:T(8,128)}, s32[4,8,2048]{2,1,0:T(8,128)S(1)}, ...), condition=%wide.region_7.8_spmd.clone, body=%wide.region_6.7_spmd.clone.sunk | while | flops 1078984832 | bytes 6063223 | solution.py:27
  218.7 0.1 constant_dynamic-slice_fusion.2
  218.8 6.0 %fusion.111 = f32[2048,256]{1,0:T(8,128)} fusion(s32[128]{0:T(128)S(1)} %iota_add_fusion.2, s32[8,2048]{1,0:T(8,128)S(1)} %dynamic-slice_bitcast_fusion.26, f32[2048,256]{1,0:T(8,128)} %get-tuple-element.436, bf16[8,2048]{1,0:T(8,128)(2,1)S(1)} %dynamic-slice_bitcast_fusion.27, pred[]{:T(512)S(6)} %compare.8, ...), kind=kOutput, calls=%fused_computation.43.clone.1 | convolution fusion | flops 1078984704 | bytes 4817409 | tf_op jit(solution)/shard_map/while/body/eval_jaxpr/prk,pkb->rb/dot_general | solution.py:23
  224.8 0.1 constant_dynamic-slice_fusion.2
  224.9 7.0 %fusion.111 = f32[2048,256]{1,0:T(8,128)} fusion(s32[128]{0:T(128)S(1)} %iota_add_fusion.2, s32[8,2048]{1,0:T(8,128)S(1)} %dynamic-slice_bitcast_fusion.26, f32[2048,256]{1,0:T(8,128)} %get-tuple-element.436, bf16[8,2048]{1,0:T(8,128)(2,1)S(1)} %dynamic-slice_bitcast_fusion.27, pred[]{:T(512)S(6)} %compare.8, ...), kind=kOutput, calls=%fused_computation.43.clone.1 | convolution fusion | flops 1078984704 | bytes 4817409 | tf_op jit(solution)/shard_map/while/body/eval_jaxpr/prk,pkb->rb/dot_general | solution.py:23
  232.0 0.1 constant_dynamic-slice_fusion.2
  232.1 7.0 %fusion.111 = f32[2048,256]{1,0:T(8,128)} fusion(s32[128]{0:T(128)S(1)} %iota_add_fusion.2, s32[8,2048]{1,0:T(8,128)S(1)} %dynamic-slice_bitcast_fusion.26, f32[2048,256]{1,0:T(8,128)} %get-tuple-element.436, bf16[8,2048]{1,0:T(8,128)(2,1)S(1)} %dynamic-slice_bitcast_fusion.27, pred[]{:T(512)S(6)} %compare.8, ...), kind=kOutput, calls=%fused_computation.43.clone.1 | convolution fusion | flops 1078984704 | bytes 4817409 | tf_op jit(solution)/shard_map/while/body/eval_jaxpr/prk,pkb->rb/dot_general | solution.py:23
  239.2 7.0 %fusion.111 = f32[2048,256]{1,0:T(8,128)} fusion(s32[128]{0:T(128)S(1)} %iota_add_fusion.2, s32[8,2048]{1,0:T(8,128)S(1)} %dynamic-slice_bitcast_fusion.26, f32[2048,256]{1,0:T(8,128)} %get-tuple-element.436, bf16[8,2048]{1,0:T(8,128)(2,1)S(1)} %dynamic-slice_bitcast_fusion.27, pred[]{:T(512)S(6)} %compare.8, ...), kind=kOutput, calls=%fused_computation.43.clone.1 | convolution fusion | flops 1078984704 | bytes 4817409 | tf_op jit(solution)/shard_map/while/body/eval_jaxpr/prk,pkb->rb/dot_general | solution.py:23
  246.2 4.6 %fusion.72 = f32[1,128,256]{2,0,1:T(1,128)S(1)} fusion(bf16[32]{0:T(256)(128)(2,1)S(1)} %copy-done, f32[32,128,256]{2,1,0:T(8,128)} %bitcast.136, f32[128]{0:T(128)S(1)} %get-tuple-element.252), kind=kOutput, calls=%fused_computation.81 | convolution fusion | flops 4194304 | bytes 4325952 | tf_op jit(solution)/shard_map/p,pik->ik/dot_general | solution.py:81
  250.8 48.0 %all-to-all-done = bf16[8,32,128,256]{3,2,1,0:T(8,128)(2,1)} async-done(((bf16[8,32,128,256]{3,2,1,0:T(8,128)(2,1)}), bf16[8,32,128,256]{3,2,1,0:T(8,128)(2,1)}, u32[]{:S(2)}, u32[]{:S(2)}) %all-to-all-start) | async-done | bytes 16777248 | tf_op jit(solution)/shard_map/all_to_all | solution.py:85
  298.9 22.6 %copy.26 = bf16[8,32,128,256]{2,3,0,1:T(8,128)(2,1)} copy(bf16[8,32,128,256]{3,2,1,0:T(8,128)(2,1)} %all-to-all-done) | data formatting | bytes 33554432 | tf_op jit(solution)/shard_map/all_to_all | solution.py:85
  321.4 23.0 %while.44 = (s32[]{:T(128)}, f32[128,256]{1,0:T(8,128)S(1)}, bf16[4,8,128,2048]{2,3,1,0:T(8,128)(2,1)}, s32[4,8,256]{2,1,0:T(8,128)S(1)}, bf16[4,8,256]{2,1,0:T(8,128)(2,1)S(1)}, /*index=5*/s32[]{:T(128)}, s32[]{:T(128)}) while((s32[]{:T(128)}, f32[128,256]{1,0:T(8,128)S(1)}, bf16[4,8,128,2048]{2,3,1,0:T(8,128)(2,1)}, ...), condition=%wide.region_5.6_spmd.clone, body=%wide.region_4.5_spmd.clone.sunk | while | flops 1082195968 | bytes 12882027 | solution.py:95
  321.4 2.6 fusion.109
  324.1 3.2 fusion.110
  327.3 2.6 fusion.109
  329.9 3.2 fusion.110
  333.1 2.5 fusion.109
  335.6 3.2 fusion.110
  338.8 2.5 fusion.109
  341.3 3.2 fusion.110
  344.5 37.4 %reduce-scatter.2.cloned.1.call-done = f32[128,256]{1,0:T(8,128)} async-done(((f32[2048,256]{1,0:T(8,128)}), f32[128,256]{1,0:T(8,128)}) %reduce-scatter.2.cloned.1.call-update) | async-done | bytes 131088 | tf_op jit(solution)/shard_map/reduce_scatter | solution.py:101
  381.9 1.6 fusion.63
  (57 shorter events, 0.5 us)
Async XLA Ops:
  6.5 70.9 %copy-start = (bf16[32]{0:T(256)(128)(2,1)S(1)}, bf16[32]{0:T(256)(128)(2,1)}, u32[]{:S(2)}) copy-start(bf16[32]{0:T(256)(128)(2,1)} %param.19) | copy-start | bytes 196
  8.5 30.7 %copy-start.1 = (bf16[128,256]{1,0:T(8,128)(2,1)}, bf16[128,256]{1,0:T(8,128)(2,1)S(1)}, u32[]{:S(2)}) copy-start(bf16[128,256]{1,0:T(8,128)(2,1)S(1)} %multiply_multiply_fusion) | copy-start | bytes 196612
  52.9 5.5 %copy-start.2 = (bf16[32,32]{1,0:T(8,128)(2,1)S(1)}, bf16[32,32]{1,0:T(8,128)(2,1)}, u32[]{:S(2)}) copy-start(bf16[32,32]{1,0:T(8,128)(2,1)} %param.18) | copy-start | bytes 6148
  52.9 5.5 %copy-start.3 = (s32[32]{0:T(128)S(1)}, s32[32]{0:T(128)}, u32[]{:S(2)}) copy-start(s32[32]{0:T(128)} %param.17) | copy-start | bytes 388
  70.6 228.3 %all-to-all-start = ((bf16[8,32,128,256]{3,2,1,0:T(8,128)(2,1)}), bf16[8,32,128,256]{3,2,1,0:T(8,128)(2,1)}, u32[]{:S(2)}, u32[]{:S(2)}) async-start(bf16[8,32,128,256]{3,2,1,0:T(8,128)(2,1)} %stack.2), calls=%async_computation | async-start | bytes 33554432 | tf_op jit(solution)/shard_map/all_to_all | solution.py:85
  76.4 122.2 %all-gather.2.cloned.1.call-start = ((), (), s32[]{:S(2)}) async-start(), calls=%async_computation.2 | async-start | bytes 1114112 | tf_op jit(solution)/shard_map/all_gather | solution.py:63
  77.1 304.8 %reduce-scatter.2.cloned.1.call-start = ((), (), s32[]{:S(2)}) async-start(), calls=%async_computation.3 | async-start | bytes 2228224 | tf_op jit(solution)/shard_map/reduce_scatter | solution.py:101
Sparse Core Ops, SparseCore 0:
  79.6 118.9 all-gather.1
  246.4 135.4 reduce-scatter.1
